TPU v7x, 128 devices: a whole 4x4x4 slice. The times are simulated.
128 devices in a mesh: dev: 2 (over y_hi), vert: 16 (over z, x), ha: 4 (over y_lo, core).
Axes of the slice: x: 4, y: 4 (y_hi: 2, y_lo: 2; y = y_hi * 2 + y_lo), z: 4, core: 2. Of those that a mesh axis runs over, the one named last changes fastest.
Arguments:
- teacher_logits: bfloat16 [2048, 128256], P(('dev', 'ha'), 'vert'), parts along dimension 0, may hold values from -40 to 260
- student_logits: bfloat16 [2048, 128256], P('dev', ('vert', 'ha')), parts along dimension 0, may hold values from -40 to 260
- targets: int32 [2048], P('dev'), parts along dimension 0, may hold values from 0 to 128255
- loss_mask: int32 [2048], P('dev'), parts along dimension 0, may hold values 0 or 1
- unembed: bfloat16 [128256, 4096], P(('vert', 'ha')), may hold values from -9 to 9
Outputs:
- hidden_grad: bfloat16 [2048, 4096], P(('dev', 'vert'), 'ha'), parts along dimension 0
There are 2 independent parts, one for each index of `dev`. A program takes and returns all parts, laid end to end along the dimension named above; an argument that names none is the same for every part. Nothing has to cross between parts.
All inputs are finite; a program needn't handle non-finite values.
Results may differ from a plain program's by a relative error of at most 0.0034.
Values may be sent and summed in bfloat16 or wider, within the bound.
A program may use at most 128 MiB of HBM per device.

v0:
```python
import jax
import jax.numpy as jnp
from jax import lax
from jax.sharding import PartitionSpec as P


def from_everyone(x, axis):
    devices = lax.axis_size(axis)
    return lax.all_to_all(jnp.broadcast_to(x[None], (devices, *x.shape)), axis, 0, 0, tiled=True)


def all_in_one(x, axis):
    leaves = jax.tree.leaves(x)
    turns = sorted(range(len(leaves)), key=lambda k: -leaves[k].size)
    width = (1, *leaves[turns[0]].shape)[-1]
    lines = [
        jnp.pad(leaves[k].reshape(-1), (0, -leaves[k].size % width)).reshape(-1, width)
        for k in turns
    ]
    both, at, found = (from_everyone(jnp.concatenate(lines), axis), 0, {})
    for k, line in zip(turns, lines):
        section = both[:, at : at + len(line)].reshape(len(both), -1)
        found[k] = section[:, : leaves[k].size].reshape(-1, *leaves[k].shape)
        at += len(line)
    numbers = iter(range(len(leaves)))
    return jax.tree.map(lambda _: found[next(numbers)], x)


def combined_pairwise(pieces, combine):
    while len(jax.tree.leaves(pieces)[0]) > 1:
        pieces = jax.vmap(combine)(
            *(jax.tree.map(lambda part: part[side::2], pieces) for side in (0, 1))
        )
    return jax.tree.map(lambda part: part[0], pieces)


def joined_all(x, axis, combine):
    pieces = all_in_one(x, axis)
    return combined_pairwise(pieces, combine)


def in_blocks(x, dim, devices):
    before, after = (x.shape[:dim], x.shape[dim + 1 :])
    return jnp.moveaxis(x.reshape(*before, devices, -1, *after), dim, 0)


def summed_on_arrival(x, axis, dim):
    tiles = in_blocks(x, dim, lax.axis_size(axis))
    arrived = lax.all_to_all(tiles, axis, split_axis=0, concat_axis=0, tiled=True)
    return arrived.sum(axis=0)


def row_stats(values):
    top = jnp.max(values, axis=1)
    return (top, jnp.sum(jnp.exp(values - top[:, None]), axis=1))


def pair_merge(first, second):
    top = jnp.maximum(first[0], second[0])
    return (top, first[1] * jnp.exp(first[0] - top) + second[1] * jnp.exp(second[0] - top))


def quad_merge(first, second):
    teach_part = pair_merge((first[0], first[1]), (second[0], second[1]))
    stud_part = pair_merge((first[2], first[3]), (second[2], second[3]))
    return (teach_part[0], teach_part[1], stud_part[0], stud_part[1])


def on_device(teacher_logits, student_logits, targets, loss_mask, unembed):
    width = student_logits.shape[1]
    offset = (lax.axis_index("vert") * lax.axis_size("ha") + lax.axis_index("ha")) * width
    stud_vals = student_logits.astype(jnp.float32)
    moved = lax.all_to_all(teacher_logits, "ha", split_axis=1, concat_axis=0, tiled=True)
    teach_vals = moved.astype(jnp.float32)
    teach_local = row_stats(teach_vals)
    stud_local = row_stats(stud_vals)
    teach_max, teach_sum, stud_max, stud_sum = joined_all(
        (teach_local[0], teach_local[1], stud_local[0], stud_local[1]), ("vert", "ha"), quad_merge
    )
    teach_lse = teach_max + jnp.log(teach_sum)
    teach_prob = jnp.exp(teach_vals - teach_lse[:, None]).astype(jnp.bfloat16)
    stud_lse = stud_max + jnp.log(stud_sum)
    stud_prob = jnp.exp(stud_vals - stud_lse[:, None])
    columns = jnp.arange(width, dtype=jnp.int32) + offset
    target_hot = (columns[None, :] == targets[:, None]).astype(jnp.float32)
    weight = loss_mask.astype(jnp.float32)[:, None]
    logit_grad = (
        (stud_prob - 0.5 * teach_prob.astype(jnp.float32) - 0.5 * target_hot) * weight
    ).astype(jnp.bfloat16)
    share = lax.psum_scatter(
        jnp.dot(logit_grad, unembed, preferred_element_type=jnp.float32),
        "vert",
        scatter_dimension=0,
        tiled=True,
    )
    result = summed_on_arrival(share, "ha", 1)
    return result.astype(jnp.bfloat16)


def solution(mesh):
    placed = (
        P(("dev", "ha"), "vert"),
        P("dev", ("vert", "ha")),
        P("dev"),
        P("dev"),
        P(("vert", "ha"), None),
    )
    return jax.shard_map(
        on_device, mesh=mesh, in_specs=placed, out_specs=P(("dev", "vert"), "ha"), check_vma=False
    )
```

profile of v0, /device:TPU:0, one launch (start us, length us, event | category | flops | bytes accessed | tf_op | source)
XLA Modules:
  0.0 264.6 jit_solution(8158680630570138530)
XLA Ops:
  6.5 3.9 %all_to_all.18 = bf16[256,4,2004]{0,2,1:T(8,128)(2,1)} reshape(bf16[256,8016]{0,1:T(8,128)(2,1)} %param.5) | data formatting | bytes 8208384 | tf_op jit(solution)/shard_map/all_to_all | solution.py:73
  10.5 4.8 %all-to-all-start = ((bf16[256,4,2004]{0,2,1:T(8,128)(2,1)}), bf16[256,4,2004]{0,2,1:T(8,128)(2,1)}, u32[]{:S(2)}, u32[]{:S(2)}) async-start(bf16[256,4,2004]{0,2,1:T(8,128)(2,1)} %all_to_all.18), calls=%async_computation | async-start | bytes 8224768 | tf_op jit(solution)/shard_map/all_to_all | solution.py:73
  15.3 6.5 %copy.15 = bf16[1024,2004]{1,0:T(8,128)(2,1)} copy(bf16[1024,2004]{0,1:T(8,128)(2,1)} %param.6) | data formatting | bytes 8208384 | tf_op args[1]
  21.8 2.9 %reduce_max.40 = bf16[1024]{0:T(1024)(128)(2,1)S(1)} reduce(bf16[1024,2004]{0,1:T(8,128)(2,1)} %param.6, bf16[]{:T(256)} %constant.8.clone.1), dimensions={1}, to_apply=%region_2.0 | reduce | flops 2051072 | bytes 4106242 | tf_op jit(solution)/shard_map/reduce_max | solution.py:54
  24.6 0.0 copy-start.1
  24.6 3.7 %fusion.1 = f32[1024]{0:T(1024)S(1)} fusion(bf16[1024,2004]{1,0:T(8,128)(2,1)} %copy.15, f32[1024]{0:T(1024)S(1)} %reduce_max.45), kind=kLoop, calls=%fused_computation.3 | loop fusion | flops 6155264 | bytes 4112384 | tf_op jit(solution)/shard_map/reduce_sum | solution.py:55
  28.3 34.3 %all-to-all-done = bf16[256,4,2004]{0,2,1:T(8,128)(2,1)} async-done(((bf16[256,4,2004]{0,2,1:T(8,128)(2,1)}), bf16[256,4,2004]{0,2,1:T(8,128)(2,1)}, u32[]{:S(2)}, u32[]{:S(2)}) %all-to-all-start) | async-done | bytes 4104224 | tf_op jit(solution)/shard_map/all_to_all | solution.py:73
  62.6 2.7 %bitcast_reduce_fusion = bf16[4,256]{1,0:T(4,128)(2,1)S(1)} fusion(bf16[256,4,2004]{0,2,1:T(8,128)(2,1)} %all-to-all-done), kind=kLoop, calls=%fused_computation.14 | loop fusion | flops 2051072 | bytes 4106240 | tf_op jit(solution)/shard_map/reduce_max | solution.py:54
  65.3 3.5 %exponential_reduce_fusion = f32[4,256]{1,0:T(4,128)S(1)} fusion(f32[4,256]{1,0:T(4,128)S(1)} %get-tuple-element.30, bf16[256,4,2004]{0,2,1:T(8,128)(2,1)} %all-to-all-done), kind=kLoop, calls=%fused_computation.12 | loop fusion | flops 6155264 | bytes 4112384 | tf_op jit(solution)/shard_map/reduce_sum | solution.py:55
  68.9 1.2 broadcast_in_dim.2
  70.1 8.9 %all-to-all-start.1 = ((f32[64,4,1024]{2,1,0:T(4,128)}), f32[64,4,1024]{2,1,0:T(4,128)S(1)}, u32[]{:S(2)}, u32[]{:S(2)}) async-start(f32[64,4,1024]{2,1,0:T(4,128)} %broadcast_in_dim.2), calls=%async_computation.1 | async-start | bytes 2097152 | tf_op jit(solution)/shard_map/all_to_all | solution.py:9
  79.0 0.2 reduce-scatter.2.cloned.1.call-start
  79.3 0.0 copy-done.1
  79.3 6.0 %bitcast_convert_fusion = f32[4,256,2004]{1,2,0:T(8,128)} fusion(bf16[256,4,2004]{0,2,1:T(8,128)(2,1)} %all-to-all-done), kind=kLoop, calls=%fused_computation.13 | loop fusion | flops 2052096 | bytes 12312576 | tf_op jit(solution)/shard_map/convert_element_type | solution.py:74
  85.3 8.7 %copy.17 = f32[4,256,2004]{2,1,0:T(8,128)} copy(f32[4,256,2004]{1,2,0:T(8,128)} %bitcast_convert_fusion) | data formatting | bytes 16416768 | tf_op jit(solution)/shard_map/convert_element_type | solution.py:74
  93.9 0.0 copy-start
  93.9 3.1 %all-to-all-done.1 = f32[64,4,1024]{2,1,0:T(4,128)S(1)} async-done(((f32[64,4,1024]{2,1,0:T(4,128)}), f32[64,4,1024]{2,1,0:T(4,128)S(1)}, u32[]{:S(2)}, u32[]{:S(2)}) %all-to-all-start.1) | async-done | bytes 1048608 | tf_op jit(solution)/shard_map/all_to_all | solution.py:9
  97.1 0.8 fusion.13
  97.8 0.1 copy_bitcast_fusion
  98.2 0.1 copy_bitcast_fusion.2
  98.4 0.1 multiply_add_fusion
  99.0 0.1 multiply_add_fusion.1
  99.7 0.0 copy-done
  99.7 7.3 %fusion.6 = bf16[1024,2004]{1,0:T(8,128)(2,1)S(1)} fusion(bf16[1024,2004]{1,0:T(8,128)(2,1)} %copy.15, f32[4,256,2004]{2,1,0:T(8,128)} %copy.17, f32[1024]{0:T(1024)S(1)} %convert_element_type.34, s32[2004]{0:T(1024)S(1)} %iota_add_fusion, f32[1024]{0:T(1024)S(1)} %bitcast.46, f32[1024]{0:T(1024)S(1)} %bitcast.47, s32[1024]{0:T(1024)S(1)} %copy-done), kind=kLoop, calls=%fused_computation.8 | loop fusion | flops 24625152 | bytes 16441168 | tf_op jit(solution)/shard_map/convert_element_type | solution.py:89
  107.0 22.2 %fusion.14 = f32[1024,4096]{1,0:T(8,128)} fusion(bf16[1024,2004]{1,0:T(8,128)(2,1)S(1)} %fusion.6, bf16[2004,4096]{1,0:T(8,128)(2,1)} %param.9), kind=kOutput, calls=%fused_computation.46 | convolution fusion | flops 16810770432 | bytes 37298176 | tf_op jit(solution)/shard_map/dot_general | solution.py:91
  129.2 0.0 reduce-scatter.2.cloned.1.call-update
  129.3 109.6 %reduce-scatter.2.cloned.1.call-done = f32[64,4096]{1,0:T(8,128)} async-done(((f32[1024,4096]{1,0:T(8,128)}), f32[64,4096]{1,0:T(8,128)}) %reduce-scatter.2.cloned.1.call-update) | async-done | bytes 1048592 | tf_op jit(solution)/shard_map/reduce_scatter | solution.py:90
  238.8 1.3 copy.32
  240.1 16.9 %all_to_all.26 = f32[4,64,1024]{2,1,0:T(8,128)S(1)} all-to-all(f32[4,64,1024]{2,1,0:T(8,128)S(1)} %bitcast.43), channel_id=1, replica_groups=mesh['dev'=2,'vert'=16,'ha'=4] {'ha'}, dimensions={0} | all-to-all | bytes 2097152 | tf_op jit(solution)/shard_map/all_to_all | solution.py:49
  257.0 0.7 reduce_sum.29
  (57 shorter events, 1.4 us)
Async XLA Ops:
  10.5 52.1 %all-to-all-start = ((bf16[256,4,2004]{0,2,1:T(8,128)(2,1)}), bf16[256,4,2004]{0,2,1:T(8,128)(2,1)}, u32[]{:S(2)}, u32[]{:S(2)}) async-start(bf16[256,4,2004]{0,2,1:T(8,128)(2,1)} %all_to_all.18), calls=%async_computation | async-start | bytes 8224768 | tf_op jit(solution)/shard_map/all_to_all | solution.py:73
  24.6 54.6 %copy-start.1 = (s32[1024]{0:T(1024)S(1)}, s32[1024]{0:T(1024)}, u32[]{:S(2)}) copy-start(s32[1024]{0:T(1024)} %param.8) | copy-start | bytes 12292
  70.1 27.0 %all-to-all-start.1 = ((f32[64,4,1024]{2,1,0:T(4,128)}), f32[64,4,1024]{2,1,0:T(4,128)S(1)}, u32[]{:S(2)}, u32[]{:S(2)}) async-start(f32[64,4,1024]{2,1,0:T(4,128)} %broadcast_in_dim.2), calls=%async_computation.1 | async-start | bytes 2097152 | tf_op jit(solution)/shard_map/all_to_all | solution.py:9
  79.0 159.8 %reduce-scatter.2.cloned.1.call-start = ((), (), s32[]{:S(2)}) async-start(), calls=%async_computation.4 | async-start | bytes 17825792 | tf_op jit(solution)/shard_map/reduce_scatter | solution.py:90
  93.9 5.8 %copy-start = (s32[1024]{0:T(1024)S(1)}, s32[1024]{0:T(1024)}, u32[]{:S(2)}) copy-start(s32[1024]{0:T(1024)} %param.7) | copy-start | bytes 12292
Sparse Core Ops, SparseCore 0:
  129.4 109.3 reduce-scatter.1
where the time goes:
time: 266 us; the launch traced here: 265 us
  waiting for transfers between devices  147 us (55%)
  other arithmetic  27.2 us (10%)
  local copies, waits for them, and re-layouts  23.7 us (9%)
  matrix products  22.2 us (8%)
  blocking collectives  16.9 us (6%)
  starting transfers between devices  13.9 us (5%)
  between operations  13.7 us (5%)
    reduce_scatter x1, waiting for transfers between devices, on_device(): lax.psum_scatter(jnp.dot(logit_grad, unembed, preferred_element_type=jnp....  110 us
    all_to_all x1, waiting for transfers between devices, on_device(): lax.all_to_all(teacher_logits, 'ha', split_axis=1, concat_axis=0, tiled=T...  34.3 us
    dot_general x1, matrix products, on_device(): jnp.dot(logit_grad, unembed, preferred_element_type=jnp.float32)  22.2 us
    all_to_all x1, blocking collectives, summed_on_arrival(): lax.all_to_all(tiles, axis, split_axis=0, concat_axis=0, tiled=True)  16.9 us
    all_to_all x1, starting transfers between devices, from_everyone(): lax.all_to_all(jnp.broadcast_to(x[None], (devices, *x.shape)), axis, 0, 0...  8.9 us
    convert_element_type x1, local copies, waits for them, and re-layouts, on_device(): teach_vals = moved.astype(jnp.float32)  8.67 us
    convert_element_type x1, other arithmetic, on_device(): logit_grad = ((stud_prob - 0.5 * teach_prob.astype(jnp.float32) - 0.5 * t...  7.26 us
    reduce_sum x2, other arithmetic, row_stats(): return (top, jnp.sum(jnp.exp(values - top[:, None]), axis=1))  7.22 us
  transfers between devices with their start and end apart: 3, of which 3 were waited for; matrix products, arithmetic and copies ran while one was open for 10% of the time, Pallas kernels for 0%

commit v1 on v0

v1 whole, which is shorter than its diff:
```python
import functools

import jax
import jax.numpy as jnp
from jax import lax
from jax.experimental import pallas as pl
from jax.experimental.pallas import tpu as pltpu
from jax.sharding import PartitionSpec as P

MESH = pl.DeviceIdType.MESH
F32, BF16 = jnp.float32, jnp.bfloat16

TOK, DIM, WIDTH = 1024, 4096, 2004
VERT, HA, SIDE = 16, 4, 4
OWN = TOK // VERT
LANES = 2048
CHUNKS = 4
RPO = OWN // CHUNKS
ROWS = RPO * VERT
SENT = ROWS // HA
HALF = DIM // 2
TILE = 256
LOW = -1e30


def body(
    teach_ref, stud_ref, targ_ref, mask_ref, emb_ref, out_ref,
    emb, exch, grad, pair_out, pair_in, part, one_out, one_in, acc_one, two_in, acc_two, last_in,
    col_top, col_sum, col_targ, col_mask, col_tlse, col_slse, msg_one, got_one, msg_two, got_two,
    emb_sem, exch_send, exch_recv, stat_send, stat_recv, pair_send, pair_recv,
    one_send, one_recv, two_send, two_recv, last_send, last_recv,
):
    vert, ha = lax.axis_index("vert"), lax.axis_index("ha")
    core, ylo = lax.rem(ha, 2), ha // 2
    zpos, xpos = vert // SIDE, lax.rem(vert, SIDE)
    apos = xpos + core * (zpos - xpos)
    bpos = zpos + core * (xpos - zpos)
    step_a, step_b = 1 + 3 * core, 4 - 3 * core

    def to_ha(d):
        return {"ha": lax.rem(ha + d, HA)}

    def to_core():
        return {"ha": ha + 1 - 2 * core}

    def to_vert(e):
        return {"vert": lax.rem(vert + e, VERT)}

    def to_a(d):
        return {"vert": lax.rem(apos + d, SIDE) * step_a + bpos * step_b}

    def to_b(d):
        return {"vert": apos * step_a + lax.rem(bpos + d, SIDE) * step_b}

    def remote(src, dst, send, recv, target):
        return pltpu.make_async_remote_copy(
            src_ref=src, dst_ref=dst, send_sem=send, recv_sem=recv, device_id=target, device_id_type=MESH
        )

    barrier = pltpu.get_barrier_semaphore()
    for e in range(1, VERT):
        pl.semaphore_signal(barrier, inc=1, device_id=to_vert(e), device_id_type=MESH)
    for d in range(1, HA):
        pl.semaphore_signal(barrier, inc=1, device_id=to_ha(d), device_id_type=MESH)

    emb_copy = pltpu.make_async_copy(emb_ref, emb, emb_sem)
    emb_copy.start()

    lane = lax.broadcasted_iota(jnp.int32, (16, LANES), 1)
    inside = lane < WIDTH

    def local_stats(values):
        top = jnp.max(values, axis=1, keepdims=True)
        return top, jnp.sum(jnp.exp(values - top), axis=1, keepdims=True)

    def keep_stats(row, top, total):
        col_top[pl.ds(row, 16), :] = jnp.broadcast_to(top, (16, 128))
        col_sum[pl.ds(row, 16), :] = jnp.broadcast_to(total, (16, 128))

    def exch_copy(c, d):
        return remote(
            exch.at[c, 3 + d], exch.at[c, d], exch_send.at[c, d], exch_recv.at[c, d], to_ha(d)
        )

    def prepare(c):
        def group(q, carry):
            row = pl.multiple_of(q * OWN + c * RPO, 16)
            tops, sums = [], []
            for j in range(HA):
                first = j * WIDTH // 128 * 128
                shift = j * WIDTH - first
                span = LANES + (128 if shift + LANES > LANES and shift else 0)
                span = min(span, 63 * 128 - first)
                values = teach_ref[pl.ds(row, 16), first : first + span].astype(F32)
                if shift:
                    values = pltpu.roll(values, span - shift, 1)[:, :LANES]
                d = lax.rem(j + HA - ha, HA)
                place = d + 3 * ((d + 3) // 4)
                exch[c, place, pl.ds(pl.multiple_of(q * RPO, 16), 16), :] = values.astype(BF16)
                top, total = local_stats(jnp.where(inside, values, LOW))
                tops.append(top)
                sums.append(total)
            top = functools.reduce(jnp.maximum, tops)
            total = sum(s * jnp.exp(t - top) for s, t in zip(sums, tops))
            keep_stats(row, top, total)
            return carry

        lax.fori_loop(0, HA, group, 0)

    prepare(0)
    pl.semaphore_wait(barrier, VERT - 1 + HA - 1)
    for d in range(1, HA):
        exch_copy(0, d).start()
    for c in range(1, CHUNKS):
        prepare(c)

    eye = lax.broadcasted_iota(jnp.int32, (128, 128), 0) == lax.broadcasted_iota(jnp.int32, (128, 128), 1)

    def packed(ref, block):
        return jnp.sum(jnp.where(eye, ref[block * 128 : block * 128 + 128, :], 0.0), axis=0, keepdims=True)

    def unpack(ref, block, line):
        column = jnp.sum(jnp.where(eye, jnp.broadcast_to(line, (128, 128)), 0.0), axis=1, keepdims=True)
        ref[block * 128 : block * 128 + 128, :] = jnp.broadcast_to(column, (128, 128))

    for block in range(2):
        msg_one[16 + block : 17 + block, :] = packed(col_top, block)
        msg_one[18 + block : 19 + block, :] = packed(col_sum, block)
    msg_one[20:24, :] = jnp.zeros((4, 128), F32)

    def stud_group(g, carry):
        row = pl.multiple_of(g * 16, 16)
        values = jnp.where(inside, stud_ref[pl.ds(row, 16), :].astype(F32), LOW)
        keep_stats(row, *local_stats(values))
        return carry

    lax.fori_loop(0, TOK // 16, stud_group, 0)
    for block in range(8):
        msg_one[block : block + 1, :] = packed(col_top, block)
        msg_one[8 + block : 9 + block, :] = packed(col_sum, block)

    def stat_one(e):
        return remote(msg_one, got_one.at[e], stat_send.at[e], stat_recv.at[e], to_vert(e))

    for e in range(1, VERT):
        stat_one(e).start()
    for block in range(8):
        unpack(col_targ, block, targ_ref[block : block + 1, :].astype(F32))
        unpack(col_mask, block, mask_ref[block : block + 1, :].astype(F32))
    for e in range(1, VERT):
        stat_one(e).wait()

    def combined(get, count):
        tops, sums = zip(*(get(e) for e in range(count)))
        top = functools.reduce(jnp.maximum, tops)
        return top, sum(s * jnp.exp(t - top) for s, t in zip(sums, tops))

    def line_of(e, first, count):
        return msg_one[first : first + count, :] if e == 0 else got_one[e, first : first + count, :]

    stud_top, stud_sum = combined(lambda e: (line_of(e, 0, 8), line_of(e, 8, 8)), VERT)
    teach_top, teach_sum = combined(lambda e: (line_of(e, 16, 2), line_of(e, 18, 2)), VERT)
    teach_lse = teach_top + jnp.log(teach_sum)
    msg_two[0:8, :] = stud_top
    msg_two[8:16, :] = stud_sum
    for k in range(4):
        msg_two[16 + 2 * k : 18 + 2 * k, :] = teach_lse
    mine = lax.broadcasted_iota(jnp.int32, (8, 128), 0) // 2 == ha
    msg_two[16:24, :] = jnp.where(mine, msg_two[16:24, :], 0.0)

    def stat_two(d):
        return remote(msg_two, got_two.at[d], stat_send.at[VERT + d], stat_recv.at[VERT + d], to_ha(d))

    for d in range(1, HA):
        stat_two(d).start()
    for c in range(1, CHUNKS):
        for d in range(1, HA):
            exch_copy(c, d).start()
    for d in range(1, HA):
        stat_two(d).wait()

    def line_two(d, first):
        return msg_two[first : first + 8, :] if d == 0 else got_two[d, first : first + 8, :]

    stud_top, stud_sum = combined(lambda d: (line_two(d, 0), line_two(d, 8)), HA)
    stud_lse = stud_top + jnp.log(stud_sum)
    teach_lse = sum(line_two(d, 16) for d in range(HA))
    for block in range(8):
        unpack(col_slse, block, stud_lse[block : block + 1, :])
        unpack(col_tlse, block, teach_lse[block : block + 1, :])
    emb_copy.wait()

    offset = (vert * HA + ha) * WIDTH

    def pair_copy(c):
        return remote(pair_out.at[c % 2], pair_in.at[c % 2], pair_send.at[c], pair_recv.at[c], to_core())

    def one_copy(c, d):
        return remote(one_out.at[c, d], one_in.at[c, d], one_send.at[c, d], one_recv.at[c, d], to_a(d))

    def two_copy(c, d):
        there = pl.multiple_of(lax.rem(bpos + d, SIDE) * RPO, RPO)
        return remote(
            acc_one.at[c, pl.ds(there, RPO)], two_in.at[c, d], two_send.at[c, d], two_recv.at[c, d], to_b(d)
        )

    def last_copy(c):
        away = pl.multiple_of((1 - ylo) * (HALF // 2), 128)
        return remote(
            acc_two.at[c, :, pl.ds(away, HALF // 2)], last_in.at[c], last_send.at[c], last_recv.at[c], to_ha(2)
        )

    def product(c, which, dst):
        def step(n, carry):
            column = which * (DIM // 4) + (n // 4) * HALF + lax.rem(n, 4) * TILE
            dst[:, pl.ds(pl.multiple_of(n * TILE, TILE), TILE)] = jnp.dot(
                grad[:, :WIDTH], emb[:, pl.ds(pl.multiple_of(column, TILE), TILE)],
                preferred_element_type=F32,
            )
            return carry

        lax.fori_loop(0, HALF // TILE, step, 0)

    def multiply(c):
        for d in range(1, HA):
            exch_copy(c, d).wait()

        def group(v, carry):
            row = pl.multiple_of(v * OWN + c * RPO, 16)
            d = lax.rem(ha + HA - v // 4, HA)
            teach = exch[c, d, pl.ds(pl.multiple_of(lax.rem(v, 4) * RPO, 16), 16), :].astype(F32)
            prob = jnp.exp(teach - col_tlse[pl.ds(row, 16), 0:1]).astype(BF16).astype(F32)
            stud = jnp.exp(stud_ref[pl.ds(row, 16), :].astype(F32) - col_slse[pl.ds(row, 16), 0:1])
            at = col_targ[pl.ds(row, 16), 0:1].astype(jnp.int32) - offset
            hot = jnp.where(lane == at, 0.5, 0.0)
            value = (stud - 0.5 * prob - hot) * col_mask[pl.ds(row, 16), 0:1]
            grad[pl.ds(pl.multiple_of(v * RPO, 16), 16), :] = jnp.where(inside, value, 0.0).astype(BF16)
            return carry

        lax.fori_loop(0, VERT, group, 0)
        if c >= 2:
            pair_copy(c - 2).wait_send()
        product(c, 1 - core, pair_out.at[c % 2])
        pair_copy(c).start()
        product(c, core, part)

    def stage_one(c):
        pair_copy(c).wait_recv()
        for d in range(SIDE):
            owner = lax.rem(apos + d, SIDE) * step_a

            def rows_of(q, carry):
                row = pl.multiple_of((owner + q * step_b) * RPO, RPO)
                value = part[pl.ds(row, RPO), :] + pair_in[c % 2, pl.ds(row, RPO), :]
                to = pl.ds(pl.multiple_of(q * RPO, RPO), RPO)
                if d == 0:
                    acc_one[c, to, :] = value
                else:
                    one_out[c, d, to, :] = value.astype(BF16)
                return carry

            lax.fori_loop(0, SIDE, rows_of, 0)
        for d in range(1, SIDE):
            one_copy(c, d).start()

    def stage_two(c):
        for d in range(1, SIDE):
            one_copy(c, d).wait_recv()

        def rows_of(q, carry):
            at = pl.ds(pl.multiple_of(q * RPO, RPO), RPO)
            acc_one[c, at, :] = acc_one[c, at, :] + sum(
                one_in[c, d, at, :].astype(F32) for d in range(1, SIDE)
            )
            return carry

        lax.fori_loop(0, SIDE, rows_of, 0)
        for d in range(1, SIDE):
            two_copy(c, d).start()

    def stage_three(c):
        for d in range(1, SIDE):
            two_copy(c, d).wait_recv()
        here = pl.ds(pl.multiple_of(bpos * RPO, RPO), RPO)
        acc_two[c] = acc_one[c, here, :] + two_in[c, 1] + two_in[c, 2] + two_in[c, 3]
        last_copy(c).start()

    def finish(c):
        last_copy(c).wait_recv()
        here = pl.ds(pl.multiple_of(ylo * (HALF // 2), 128), HALF // 2)
        out_ref[c * RPO : c * RPO + RPO, :] = (acc_two[c, :, here] + last_in[c]).astype(BF16)

    for turn in range(CHUNKS + 3):
        if turn < CHUNKS:
            multiply(turn)
            stage_one(turn)
        if 0 <= turn - 1 < CHUNKS:
            stage_two(turn - 1)
        if 0 <= turn - 2 < CHUNKS:
            stage_three(turn - 2)
        if 0 <= turn - 3 < CHUNKS:
            finish(turn - 3)

    for c in range(CHUNKS):
        if c >= CHUNKS - 2:
            pair_copy(c).wait_send()
        for d in range(1, SIDE):
            one_copy(c, d).wait_send()
            two_copy(c, d).wait_send()
        last_copy(c).wait_send()


def on_device(teacher_logits, student_logits, targets, loss_mask, unembed):
    whole = lambda shape: pl.BlockSpec(shape, lambda i: (0,) * len(shape), pipeline_mode=pl.Buffered(1))
    dma = pltpu.SemaphoreType.DMA
    scratch = [
        pltpu.VMEM((WIDTH, DIM), BF16),
        pltpu.VMEM((CHUNKS, 7, SENT, LANES), BF16),
        pltpu.VMEM((ROWS, LANES), BF16),
        pltpu.VMEM((2, ROWS, HALF), F32),
        pltpu.VMEM((2, ROWS, HALF), F32),
        pltpu.VMEM((ROWS, HALF), F32),
        pltpu.VMEM((CHUNKS, SIDE, SIDE * RPO, HALF), BF16),
        pltpu.VMEM((CHUNKS, SIDE, SIDE * RPO, HALF), BF16),
        pltpu.VMEM((CHUNKS, SIDE * RPO, HALF), F32),
        pltpu.VMEM((CHUNKS, SIDE, RPO, HALF), F32),
        pltpu.VMEM((CHUNKS, RPO, HALF), F32),
        pltpu.VMEM((CHUNKS, RPO, HALF // 2), F32),
        *[pltpu.VMEM((TOK, 128), F32)] * 6,
        pltpu.VMEM((24, 128), F32),
        pltpu.VMEM((VERT, 24, 128), F32),
        pltpu.VMEM((24, 128), F32),
        pltpu.VMEM((HA, 24, 128), F32),
        dma,
        dma((CHUNKS, HA)), dma((CHUNKS, HA)),
        dma((VERT + HA,)), dma((VERT + HA,)),
        dma((CHUNKS,)), dma((CHUNKS,)),
        dma((CHUNKS, SIDE)), dma((CHUNKS, SIDE)),
        dma((CHUNKS, SIDE)), dma((CHUNKS, SIDE)),
        dma((CHUNKS,)), dma((CHUNKS,)),
    ]
    return pl.pallas_call(
        body,
        grid=(1,),
        out_shape=jax.ShapeDtypeStruct((OWN, DIM // HA), BF16),
        in_specs=[
            whole((TOK // HA, 63 * 128)),
            whole((TOK, LANES)),
            whole((8, 128)),
            whole((8, 128)),
            pl.BlockSpec(memory_space=pl.ANY),
        ],
        out_specs=pl.BlockSpec((OWN, DIM // HA), lambda i: (0, 0)),
        scratch_shapes=scratch,
        compiler_params=pltpu.CompilerParams(
            collective_id=0, has_side_effects=True, vmem_limit_bytes=67043328
        ),
    )(teacher_logits, student_logits, targets.reshape(8, 128), loss_mask.reshape(8, 128), unembed)


def solution(mesh):
    placed = (
        P(("dev", "ha"), "vert"),
        P("dev", ("vert", "ha")),
        P("dev"),
        P("dev"),
        P(("vert", "ha"), None),
    )
    return jax.shard_map(
        on_device, mesh=mesh, in_specs=placed, out_specs=P(("dev", "vert"), "ha"), check_vma=False
    )
```

time: 266 us -> 116 us (0.44)
  waiting for transfers between devices: 147 us -> 0 us
  Pallas kernels: 0 us -> 101 us
  other arithmetic: 27.2 us -> 0 us
  matrix products: 22.2 us -> 0 us
  blocking collectives: 16.9 us -> 0 us
  starting transfers between devices: 13.9 us -> 0 us
  between operations: 13.7 us -> 0.01 us
  local copies, waits for them, and re-layouts: 23.7 us -> 14.5 us
    reduce_scatter x1 -> x0, waiting for transfers between devices: 110 us -> none  [on_device(): lax.psum_scatter(jnp.dot(logit_grad, unembed, preferred_element_type=jnp....]
    pallas_call x0 -> x1, Pallas kernels: none -> 101 us  [on_device(): pl.pallas_call(body, grid=(1,), out_shape=jax.ShapeDtypeStruct((OWN, DIM...]
    all_to_all x2 -> x0, waiting for transfers between devices: 37.4 us -> none  [the longest x1 34.3 us: on_device(): lax.all_to_all(teacher_logits, 'ha', split_axis=1, concat_axis=0, tiled=T...]
    dot_general x1 -> x0, matrix products: 22.2 us -> none  [on_device(): jnp.dot(logit_grad, unembed, preferred_element_type=jnp.float32)]
    all_to_all x1 -> x0, blocking collectives: 16.9 us -> none  [summed_on_arrival(): lax.all_to_all(tiles, axis, split_axis=0, concat_axis=0, tiled=True)]
    all_to_all x2 -> x0, starting transfers between devices: 13.7 us -> none  [the longest x1 8.9 us: from_everyone(): lax.all_to_all(jnp.broadcast_to(x[None], (devices, *x.shape)), axis, 0, 0...]
    convert_element_type x3 -> x0, other arithmetic: 13.2 us -> none  [the longest x1 7.26 us: on_device(): logit_grad = ((stud_prob - 0.5 * teach_prob.astype(jnp.float32) - 0.5 * t...]
    convert_element_type x1 -> x0, local copies, waits for them, and re-layouts: 8.67 us -> none  [on_device(): teach_vals = moved.astype(jnp.float32)]
  transfers between devices with their start and end apart: 3 -> 0, of which waited for: 3 -> 0; matrix products, arithmetic and copies ran while one was open for 10% -> 0% of each run, Pallas kernels for 0% -> 0%
where the time goes in v1:
time: 116 us
  Pallas kernels  101 us (87%)
  local copies, waits for them, and re-layouts  14.5 us (12%)
    pallas_call x1, Pallas kernels, on_device(): pl.pallas_call(body, grid=(1,), out_shape=jax.ShapeDtypeStruct((OWN, DIM...  101 us
    unnamed x3, local copies, waits for them, and re-layouts  14.5 us

profile of v1, /device:TPU:0, one launch (start us, length us, event | category | flops | bytes accessed | tf_op | source)
XLA Modules:
  0.0 115.6 jit_solution(418435994353890252)
XLA Ops:
  0.0 6.4 %copy.6.teach_ref = bf16[256,8016]{1,0:T(8,128)(2,1)} copy(bf16[256,8016]{0,1:T(8,128)(2,1)} %param.5) | data formatting | bytes 8208384 | tf_op args[0]
  6.4 6.5 %copy.7.stud_ref = bf16[1024,2004]{1,0:T(8,128)(2,1)} copy(bf16[1024,2004]{0,1:T(8,128)(2,1)} %param.6) | data formatting | bytes 8208384 | tf_op args[1]
  12.9 101.1 %shard_map.55 = bf16[64,1024]{1,0:T(8,128)(2,1)} custom-call(bf16[256,8016]{1,0:T(8,128)(2,1)} %copy.6.teach_ref, bf16[1024,2004]{1,0:T(8,128)(2,1)} %copy.7.stud_ref, s32[8,128]{1,0:T(8,128)} %bitcast.2, s32[8,128]{1,0:T(8,128)} %bitcast.3, bf16[2004,4096]{1,0:T(8,128)(2,1)} %emb_ref.1), custom_call_target="tpu_custom_call" | custom-call | tf_op jit(solution)/shard_map/pallas_call | solution.py:342
  114.1 1.6 %copy.9 = bf16[64,1024]{1,0:T(8,128)(2,1)} copy(bf16[64,1024]{1,0:T(8,128)(2,1)} %shard_map.55) | data formatting | bytes 262144
